TPU v7x, 32 devices: a whole 2x2x4 slice. The times are simulated.
32 devices in a mesh: lat: 8 (over z, y), chan: 4 (over x, core).
Axes of the slice: x: 2, y: 2, z: 4, core: 2. Of those that a mesh axis runs over, the one named last changes fastest.
Arguments:
- grid_in: bfloat16 [256, 384, 1024], P('chan', 'lat'), may hold values from -6 to 6
- quad_weights: float32 [384], P('lat'), may hold values from 0.5 to 2
- legendre: bfloat16 [384, 384, 384], P('lat'), as said below
- mixing: bfloat16 [2, 384, 256, 256], P(None, 'lat', 'chan'), may hold values from -0.375 to 0.375
Outputs:
- grid_out: bfloat16 [256, 384, 1024], P('chan', 'lat')
Inputs may be any that keep to these rules, and one draw needn't show every extreme that they name: legendre[m, l, t] is zero wherever l < m.
All inputs are finite; a program needn't handle non-finite values.
Results may differ from a plain program's by a relative error of at most 0.0068.
Values may be sent and summed in bfloat16 or wider, within the bound.
A program may use at most 128 MiB of HBM per device.

v0:
```python
import math
import jax
import jax.numpy as jnp
from jax import lax
from jax.sharding import PartitionSpec as P

M = 384


def fourier_table(number, length):
    orders = jnp.arange(number, dtype=jnp.int32)
    points = jnp.arange(length, dtype=jnp.int32)
    phases = orders[:, None] * points[None, :] % length
    angles = phases.astype(jnp.float32) * (2.0 * math.pi / length)
    factor = 1.0 / math.sqrt(length)
    return jnp.stack([jnp.cos(angles) * factor, -jnp.sin(angles) * factor]).astype(jnp.bfloat16)


def body(grid_in, quad_weights, legendre, mixing):
    groups = grid_in.shape[0]
    rows_lat = grid_in.shape[1]
    length = grid_in.shape[2]
    fourier = fourier_table(M, length)
    spectra = jnp.einsum("ctn,rmn->mtrc", grid_in, fourier, preferred_element_type=jnp.float32)
    spectra = spectra * quad_weights[None, :, None, None]
    weighted = spectra.astype(jnp.bfloat16).reshape(M, rows_lat, 2 * groups)
    coeffs = jnp.einsum(
        "mlt,mtk->mlk",
        legendre,
        lax.all_to_all(weighted, "lat", split_axis=0, concat_axis=1, tiled=True),
        preferred_element_type=jnp.float32,
    ).astype(jnp.bfloat16)
    by_degree = lax.all_to_all(coeffs, "lat", split_axis=1, concat_axis=0, tiled=True)
    orders = by_degree.shape[0]
    degrees = by_degree.shape[1]
    weights_out = lax.all_to_all(mixing, "chan", split_axis=3, concat_axis=2, tiled=True)
    block_in = lax.all_gather(by_degree, "chan", axis=2, tiled=True)
    shards = block_in.shape[2] // (2 * groups)
    halves = block_in.reshape(orders, degrees, shards, 2, groups)
    real_in = halves[:, :, :, 0, :].reshape(orders, degrees, shards * groups)
    imag_in = halves[:, :, :, 1, :].reshape(orders, degrees, shards * groups)
    real_weight = weights_out[0]
    imag_weight = weights_out[1]
    real_sum = jnp.einsum(
        "mlc,lcd->mld", real_in, real_weight, preferred_element_type=jnp.float32
    ) - jnp.einsum("mlc,lcd->mld", imag_in, imag_weight, preferred_element_type=jnp.float32)
    imag_sum = jnp.einsum(
        "mlc,lcd->mld", imag_in, real_weight, preferred_element_type=jnp.float32
    ) + jnp.einsum("mlc,lcd->mld", real_in, imag_weight, preferred_element_type=jnp.float32)
    mixed_coef = (
        jnp.stack([real_sum, imag_sum], axis=2)
        .reshape(orders, degrees, 2 * groups)
        .astype(jnp.bfloat16)
    )
    synthesis = jnp.einsum(
        "mlt,mlk->mtk",
        legendre,
        lax.all_to_all(mixed_coef, "lat", split_axis=0, concat_axis=1, tiled=True),
        preferred_element_type=jnp.float32,
    ).astype(jnp.bfloat16)
    gridded = lax.all_to_all(synthesis, "lat", split_axis=1, concat_axis=0, tiled=True)
    spread = gridded.reshape(M, rows_lat, 2, groups)
    restored = jnp.einsum("mtrc,rmn->ctn", spread, fourier, preferred_element_type=jnp.float32)
    return (restored + grid_in.astype(jnp.float32)).astype(jnp.bfloat16)


def solution(mesh):
    return jax.shard_map(
        body,
        mesh=mesh,
        in_specs=(
            P("chan", "lat", None),
            P("lat"),
            P("lat", None, None),
            P(None, "lat", "chan", None),
        ),
        out_specs=P("chan", "lat", None),
        check_vma=False,
    )
```

profile of v0, /device:TPU:0, one launch (start us, length us, event | category | flops | bytes accessed | tf_op | source)
XLA Modules:
  0.0 787.2 jit_solution(417036485185853445)
XLA Ops:
  6.5 0.0 all-gather.2.cloned.1.call-start
  6.5 6.4 multiply_convert_fusion.1
  13.0 0.0 copy-start.4
  13.0 0.0 copy-start.6
  13.0 0.9 copy-done.4
  13.9 0.3 copy-done.6
  14.1 15.9 %fusion.4 = bf16[384,48,2,64]{0,3,1,2:T(8,128)(2,1)S(1)} fusion(f32[48]{0:T(128)} %param.5, bf16[64,48,1024]{2,1,0:T(8,128)(2,1)} %param.4, bf16[1,384,1024]{2,1,0:T(8,128)(2,1)S(1)} %get-tuple-element.9, bf16[1,384,1024]{2,1,0:T(8,128)(2,1)S(1)} %get-tuple-element.10), kind=kOutput, calls=%fused_computation.7 | convolution fusion | flops 4839702528 | bytes 12583104 | tf_op jit(solution)/shard_map/ctn,rmn->mtrc/dot_general | solution.py:24
  30.0 2.7 copy.33
  32.8 7.0 copy.34
  39.7 111.9 %all_to_all.84 = bf16[384,48,128]{2,1,0:T(8,128)(2,1)S(1)} all-to-all(bf16[384,48,128]{2,1,0:T(8,128)(2,1)} %copy.34), channel_id=1, replica_groups=mesh['lat'=8,'chan'=4] {'lat'}, dimensions={0} | all-to-all | bytes 9437184 | tf_op jit(solution)/shard_map/all_to_all | solution.py:30
  151.6 1.4 copy.35
  153.0 9.2 %convert_bitcast_fusion.1 = bf16[48,384,128]{1,2,0:T(8,128)(2,1)} fusion(bf16[48,384,128]{2,1,0:T(8,128)(2,1)S(1)} %bitcast.87, bf16[48,384,384]{2,1,0:T(8,128)(2,1)} %param.6), kind=kOutput, calls=%fused_computation.12 | convolution fusion | flops 1814298624 | bytes 23592960 | tf_op jit(solution)/shard_map/mlt,mtk->mlk/dot_general | solution.py:27
  162.1 7.0 copy.37
  169.1 107.9 %all_to_all.85 = bf16[48,384,128]{2,0,1:T(8,128)(2,1)S(1)} all-to-all(bf16[48,384,128]{2,0,1:T(8,128)(2,1)} %copy.37), channel_id=1, replica_groups=mesh['lat'=8,'chan'=4] {'lat'}, dimensions={1} | all-to-all | bytes 9437184 | tf_op jit(solution)/shard_map/all_to_all | solution.py:33
  277.0 3.4 copy.39
  280.4 0.0 all-gather.2.cloned.1.call-update
  280.4 1.9 copy-done.3
  282.3 9.4 %copy.41 = bf16[2,48,64,256]{2,1,0,3:T(8,128)(2,1)} copy(bf16[2,48,64,256]{3,2,1,0:T(8,128)(2,1)S(1)} %copy-done.3) | data formatting | bytes 6291456 | tf_op args[3]
  291.7 7.2 reshape.101
  299.0 74.6 %all_to_all.86 = bf16[4,2,196608]{2,1,0:T(2,128)(2,1)} all-to-all(bf16[4,2,196608]{2,1,0:T(2,128)(2,1)S(1)} %reshape.101), channel_id=1, replica_groups=mesh['lat'=8,'chan'=4] {'chan'}, dimensions={0} | all-to-all | bytes 6291456 | tf_op jit(solution)/shard_map/all_to_all | solution.py:36
  373.5 7.5 reshape.102
  381.0 8.2 %copy.77 = bf16[2,48,64,4,64]{2,3,4,1,0:T(4,128)(2,1)S(1)} copy(bf16[2,48,64,4,64]{2,1,0,4,3:T(8,128)(2,1)} %bitcast.89) | data formatting | bytes 6291456 | tf_op jit(solution)/shard_map/all_to_all | solution.py:36
  389.2 4.3 fusion.20
  393.6 5.9 squeeze.7
  399.4 0.0 copy-done.1
  399.4 2.9 squeeze.6
  402.4 33.2 %all-gather.2.cloned.1.call-done = bf16[384,48,512]{2,1,0:T(8,128)(2,1)} async-done(((bf16[384,48,128]{2,1,0:T(8,128)(2,1)}), bf16[384,48,512]{2,1,0:T(8,128)(2,1)}) %all-gather.2.cloned.1.call-update) | async-done | bytes 18874384 | tf_op jit(solution)/shard_map/all_gather | solution.py:37
  435.6 25.8 %copy.40 = bf16[384,48,512]{0,2,1:T(8,128)(2,1)} copy(bf16[384,48,512]{2,1,0:T(8,128)(2,1)} %all-gather.2.cloned.1.call-done) | data formatting | bytes 37748736 | tf_op jit(solution)/shard_map/all_gather | solution.py:37
  461.4 8.5 %fusion.19 = (bf16[384,48,4,1,64]{0,4,3,2,1:T(8,128)(2,1)S(1)}, bf16[384,48,4,1,64]{0,4,3,2,1:T(8,128)(2,1)S(1)}) fusion(bf16[384,48,4,2,64]{0,4,3,2,1:T(8,128)(2,1)} %bitcast.85), kind=kLoop, calls=%fused_computation.31 | loop fusion | bytes 37748736 | tf_op jit(solution)/shard_map/slice | solution.py:40
  469.9 0.0 copy-done
  469.9 1.5 fusion.21
  471.5 1.5 fusion.22
  473.0 4.7 fusion.7
  477.7 3.4 fusion.8
  481.1 0.0 copy-done.2
  481.1 0.5 pad_maximum_fusion
  481.6 2.7 copy.47
  484.4 7.0 copy.48
  491.3 110.3 %all_to_all.87 = bf16[384,48,128]{2,1,0:T(8,128)(2,1)S(1)} all-to-all(bf16[384,48,128]{2,1,0:T(8,128)(2,1)} %copy.48), channel_id=1, replica_groups=mesh['lat'=8,'chan'=4] {'lat'}, dimensions={0} | all-to-all | bytes 9437184 | tf_op jit(solution)/shard_map/all_to_all | solution.py:58
  601.6 1.4 copy.49
  603.0 10.5 %convert_bitcast_fusion = bf16[48,384,128]{1,2,0:T(8,128)(2,1)} fusion(bf16[48,384,128]{2,1,0:T(8,128)(2,1)S(1)} %bitcast.86, bf16[48,384,384]{2,1,0:T(8,128)(2,1)} %param.6), kind=kOutput, calls=%fused_computation.9 | convolution fusion | flops 1814298624 | bytes 23592960 | tf_op jit(solution)/shard_map/mlt,mlk->mtk/dot_general | solution.py:55
  613.5 7.0 copy.51
  620.5 108.6 %all_to_all.88 = bf16[48,384,128]{2,0,1:T(8,128)(2,1)} all-to-all(bf16[48,384,128]{2,0,1:T(8,128)(2,1)} %copy.51), channel_id=1, replica_groups=mesh['lat'=8,'chan'=4] {'lat'}, dimensions={1} | all-to-all | bytes 9437184 | tf_op jit(solution)/shard_map/all_to_all | solution.py:61
  729.1 12.4 %copy.67 = bf16[8,48,48,128]{1,0,3,2:T(8,128)(2,1)} copy(bf16[8,48,48,128]{3,1,2,0:T(8,128)(2,1)} %bitcast.97) | data formatting | bytes 9437184 | tf_op jit(solution)/shard_map/reshape | solution.py:62
  741.5 16.9 %reshape.100 = bf16[384,48,2,64]{0,3,2,1:T(8,128)(2,1)} reshape(bf16[8,48,48,128]{1,0,3,2:T(8,128)(2,1)} %copy.67) | data formatting | bytes 9437184 | tf_op jit(solution)/shard_map/reshape | solution.py:62
  758.4 0.0 copy-done.5
  758.4 15.5 %fusion = bf16[64,48,1024]{2,0,1:T(8,128)(2,1)S(1)} fusion(bf16[64,48,1024]{2,1,0:T(8,128)(2,1)} %param.4, bf16[384,48,2,64]{0,3,2,1:T(8,128)(2,1)} %reshape.100, bf16[1,384,1024]{2,1,0:T(8,128)(2,1)S(1)} %copy-done.5, bf16[1,384,1024]{2,1,0:T(8,128)(2,1)S(1)} %copy-done.7), kind=kOutput, calls=%fused_computation.1 | convolution fusion | flops 4844421120 | bytes 18874368 | tf_op jit(solution)/shard_map/mtrc,rmn->ctn/dot_general | solution.py:63
  773.9 6.2 copy.56
  (7 shorter events, 0.0 us)
Async XLA Ops:
  6.5 429.0 %all-gather.2.cloned.1.call-start = ((), (), s32[]{:S(2)}) async-start(), calls=%async_computation.5 | async-start | bytes 23592960 | tf_op jit(solution)/shard_map/all_gather | solution.py:37
  13.0 0.9 copy-start.4
  13.0 1.1 copy-start.6
  280.4 1.9 copy-start.3
  393.6 5.9 copy-start.1
  461.3 8.6 %copy-start = (bf16[48,256,64]{1,2,0:T(8,128)(2,1)S(1)}, bf16[48,256,64]{1,2,0:T(8,128)(2,1)}, u32[]{:S(2)}) copy-start(bf16[48,256,64]{1,2,0:T(8,128)(2,1)} %squeeze.6) | copy-start | bytes 4718596
  477.7 3.4 copy-start.2
  741.5 16.9 %copy-start.5 = (bf16[1,384,1024]{2,1,0:T(8,128)(2,1)S(1)}, bf16[1,384,1024]{2,1,0:T(8,128)(2,1)}, u32[]{:S(2)}) copy-start(bf16[1,384,1024]{2,1,0:T(8,128)(2,1)} %copy-done.4) | copy-start | bytes 2359300
  741.5 16.9 %copy-start.7 = (bf16[1,384,1024]{2,1,0:T(8,128)(2,1)S(1)}, bf16[1,384,1024]{2,1,0:T(8,128)(2,1)}, u32[]{:S(2)}) copy-start(bf16[1,384,1024]{2,1,0:T(8,128)(2,1)} %copy-done.6) | copy-start | bytes 2359300
Sparse Core Ops, SparseCore 0:
  280.5 154.9 all-gather.1
where the time goes:
time: 796 us; the launch traced here: 787 us
  blocking collectives  513 us (64%)
  local copies, waits for them, and re-layouts  158 us (20%)
  matrix products  62.2 us (8%)
  waiting for transfers between devices  33.2 us (4%)
  between operations  13.7 us (2%)
    all_to_all x1, blocking collectives, body(): lax.all_to_all(weighted, 'lat', split_axis=0, concat_axis=1, tiled=True)  112 us
    all_to_all x1, blocking collectives, body(): lax.all_to_all(mixed_coef, 'lat', split_axis=0, concat_axis=1, tiled=True)  110 us
    all_to_all x1, blocking collectives, body(): lax.all_to_all(synthesis, 'lat', split_axis=1, concat_axis=0, tiled=True)  109 us
    all_to_all x1, blocking collectives, body(): lax.all_to_all(coeffs, 'lat', split_axis=1, concat_axis=0, tiled=True)  108 us
    all_to_all x1, blocking collectives, body(): lax.all_to_all(mixing, 'chan', split_axis=3, concat_axis=2, tiled=True)  74.6 us
    all_gather x1, waiting for transfers between devices, body(): block_in = lax.all_gather(by_degree, 'chan', axis=2, tiled=True)  33.2 us
    reshape x2, local copies, waits for them, and re-layouts, body(): spread = gridded.reshape(M, rows_lat, 2, groups)  29.3 us
    unnamed x19, local copies, waits for them, and re-layouts  27.2 us
  transfers between devices with their start and end apart: 1, of which 1 were waited for; matrix products, arithmetic and copies ran while one was open for 6% of the time, Pallas kernels for 0%

commit v1 on v0

--- a/solution.py
+++ b/solution.py
@@ -34,7 +34,12 @@
     orders = by_degree.shape[0]
     degrees = by_degree.shape[1]
     weights_out = lax.all_to_all(mixing, "chan", split_axis=3, concat_axis=2, tiled=True)
-    block_in = lax.all_gather(by_degree, "chan", axis=2, tiled=True)
+    ring = [by_degree]
+    for hop in range(3):
+        ring.append(lax.ppermute(ring[-1], "chan", [(dev, (dev + 1) % 4) for dev in range(4)]))
+    block_in = jnp.roll(
+        jnp.concatenate(ring[::-1], axis=2), (lax.axis_index("chan") + 1) * ring[0].shape[2], axis=2
+    )
     shards = block_in.shape[2] // (2 * groups)
     halves = block_in.reshape(orders, degrees, shards, 2, groups)
     real_in = halves[:, :, :, 0, :].reshape(orders, degrees, shards * groups)

time: 796 us -> 893 us (1.12)
  waiting for transfers between devices: 33.2 us -> 165 us
  blocking collectives: 513 us -> 435 us
  local copies, waits for them, and re-layouts: 158 us -> 209 us
  between operations: 13.7 us -> 0.43 us
    ppermute x0 -> x3, waiting for transfers between devices: none -> 107 us  [body(): lax.ppermute(ring[-1], 'chan', [(dev, (dev + 1) % 4) for dev in range(4)])]
    all_to_all x1 -> x0, blocking collectives: 74.6 us -> none  [body(): lax.all_to_all(mixing, 'chan', split_axis=3, concat_axis=2, tiled=True)]
    all_to_all x0 -> x1, waiting for transfers between devices: none -> 57.9 us  [body(): lax.all_to_all(mixing, 'chan', split_axis=3, concat_axis=2, tiled=True)]
    dynamic_slice x0 -> x2, local copies, waits for them, and re-layouts: none -> 41.1 us  [body(): jnp.roll(jnp.concatenate(ring[::-1], axis=2), (lax.axis_index('chan') + 1...]
    all_gather x1 -> x0, waiting for transfers between devices: 33.2 us -> none  [body(): block_in = lax.all_gather(by_degree, 'chan', axis=2, tiled=True)]
    unnamed x19 -> x36, local copies, waits for them, and re-layouts: 27.2 us -> 59.5 us
    all_gather x1 -> x0, local copies, waits for them, and re-layouts: 25.8 us -> none  [body(): block_in = lax.all_gather(by_degree, 'chan', axis=2, tiled=True)]
  transfers between devices with their start and end apart: 1 -> 4, of which waited for: 1 -> 3; matrix products, arithmetic and copies ran while one was open for 6% -> 5% of each run, Pallas kernels for 0% -> 0%
where the time goes in v1:
time: 893 us; the launch traced here: 883 us
  blocking collectives  435 us (49%)
  local copies, waits for them, and re-layouts  209 us (23%)
  waiting for transfers between devices  165 us (18%)
  matrix products  62.2 us (7%)
    all_to_all x1, blocking collectives, body(): lax.all_to_all(weighted, 'lat', split_axis=0, concat_axis=1, tiled=True)  112 us
    all_to_all x1, blocking collectives, body(): lax.all_to_all(synthesis, 'lat', split_axis=1, concat_axis=0, tiled=True)  109 us
    all_to_all x1, blocking collectives, body(): lax.all_to_all(coeffs, 'lat', split_axis=1, concat_axis=0, tiled=True)  108 us
    ppermute x3, waiting for transfers between devices, body(): lax.ppermute(ring[-1], 'chan', [(dev, (dev + 1) % 4) for dev in range(4)])  107 us
    all_to_all x1, blocking collectives, body(): lax.all_to_all(mixed_coef, 'lat', split_axis=0, concat_axis=1, tiled=True)  106 us
    unnamed x36, local copies, waits for them, and re-layouts  59.5 us
    all_to_all x1, waiting for transfers between devices, body(): lax.all_to_all(mixing, 'chan', split_axis=3, concat_axis=2, tiled=True)  57.9 us
    dynamic_slice x2, local copies, waits for them, and re-layouts, body(): jnp.roll(jnp.concatenate(ring[::-1], axis=2), (lax.axis_index('chan') + 1...  41.1 us
  transfers between devices with their start and end apart: 4, of which 3 were waited for; matrix products, arithmetic and copies ran while one was open for 5% of the time, Pallas kernels for 0%

profile of v1, /device:TPU:0, one launch (start us, length us, event | category | flops | bytes accessed | tf_op | source)
XLA Modules:
  0.0 883.0 jit_solution(2428479887195991987)
XLA Ops:
  0.0 6.4 multiply_convert_fusion.1
  7.6 15.9 %fusion.4 = bf16[384,48,2,64]{0,3,1,2:T(8,128)(2,1)S(1)} fusion(f32[48]{0:T(128)} %param.5, bf16[64,48,1024]{2,1,0:T(8,128)(2,1)} %param.4, bf16[1,384,1024]{2,1,0:T(8,128)(2,1)S(1)} %get-tuple-element.9, bf16[1,384,1024]{2,1,0:T(8,128)(2,1)S(1)} %get-tuple-element.10), kind=kOutput, calls=%fused_computation.7 | convolution fusion | flops 4839702528 | bytes 12583104 | tf_op jit(solution)/shard_map/ctn,rmn->mtrc/dot_general | solution.py:24
  23.5 2.7 copy.33
  26.2 7.0 copy.34
  33.2 111.9 %all_to_all.84 = bf16[384,48,128]{2,1,0:T(8,128)(2,1)S(1)} all-to-all(bf16[384,48,128]{2,1,0:T(8,128)(2,1)} %copy.34), channel_id=1, replica_groups=mesh['lat'=8,'chan'=4] {'lat'}, dimensions={0} | all-to-all | bytes 9437184 | tf_op jit(solution)/shard_map/all_to_all | solution.py:30
  145.1 1.4 copy.35
  146.5 9.2 %convert_bitcast_fusion.1 = bf16[48,384,128]{1,2,0:T(8,128)(2,1)} fusion(bf16[48,384,128]{2,1,0:T(8,128)(2,1)S(1)} %bitcast.92, bf16[48,384,384]{2,1,0:T(8,128)(2,1)} %param.6), kind=kOutput, calls=%fused_computation.12 | convolution fusion | flops 1814298624 | bytes 23592960 | tf_op jit(solution)/shard_map/mlt,mtk->mlk/dot_general | solution.py:27
  155.6 7.0 copy.37
  162.6 107.9 %all_to_all.85 = bf16[48,384,128]{2,0,1:T(8,128)(2,1)S(1)} all-to-all(bf16[48,384,128]{2,0,1:T(8,128)(2,1)} %copy.37), channel_id=1, replica_groups=mesh['lat'=8,'chan'=4] {'lat'}, dimensions={1} | all-to-all | bytes 9437184 | tf_op jit(solution)/shard_map/all_to_all | solution.py:33
  271.7 2.1 copy-done
  273.8 53.5 %collective-permute-done = bf16[384,48,128]{2,1,0:T(8,128)(2,1)S(1)} collective-permute-done((bf16[384,48,128]{2,1,0:T(8,128)(2,1)S(1)}, bf16[384,48,128]{2,1,0:T(8,128)(2,1)S(1)}, u32[]{:S(2)}, u32[]{:S(2)}) %collective-permute-start) | collective-permute-done | bytes 4718624 | tf_op jit(solution)/shard_map/ppermute | solution.py:39
  327.4 2.1 copy-done.2
  329.5 53.6 %collective-permute-done.1 = bf16[384,48,128]{2,1,0:T(8,128)(2,1)} collective-permute-done((bf16[384,48,128]{2,1,0:T(8,128)(2,1)S(1)}, bf16[384,48,128]{2,1,0:T(8,128)(2,1)}, u32[]{:S(2)}, u32[]{:S(2)}) %collective-permute-start.1) | collective-permute-done | bytes 4718624 | tf_op jit(solution)/shard_map/ppermute | solution.py:39
  383.2 9.4 %copy.41 = bf16[2,48,64,256]{2,1,0,3:T(8,128)(2,1)} copy(bf16[2,48,64,256]{3,2,1,0:T(8,128)(2,1)S(1)} %copy-done.4) | data formatting | bytes 6291456 | tf_op args[3]
  392.6 7.8 reshape.101
  400.4 3.9 all-to-all-start.2
  404.3 57.9 %all-to-all-done.2 = bf16[4,2,196608]{2,1,0:T(2,128)(2,1)S(1)} async-done(((bf16[4,2,196608]{2,1,0:T(2,128)(2,1)}), bf16[4,2,196608]{2,1,0:T(2,128)(2,1)S(1)}, u32[]{:S(2)}, u32[]{:S(2)}) %all-to-all-start.2) | async-done | bytes 3145760 | tf_op jit(solution)/shard_map/all_to_all | solution.py:36
  462.2 5.3 reshape.102
  467.5 7.6 copy.77
  475.1 4.4 fusion.20
  479.5 5.7 squeeze.6
  485.2 6.2 squeeze.7
  491.4 5.6 constant_dynamic-update-slice_fusion.7
  497.0 5.6 constant_dynamic-update-slice_fusion.6
  502.6 3.2 constant_dynamic-update-slice_fusion.5
  505.8 3.2 constant_dynamic-update-slice_fusion.4
  508.9 5.5 constant_dynamic-update-slice_fusion.3
  514.5 5.5 constant_dynamic-update-slice_fusion.2
  519.9 3.2 constant_dynamic-update-slice_fusion.1
  523.1 3.2 constant_dynamic-update-slice_fusion
  526.3 16.8 %constant_dynamic-slice_fusion = bf16[384,48,512]{2,1,0:T(8,128)(2,1)} fusion(bf16[384,48,1024]{2,1,0:T(8,128)(2,1)} %constant_dynamic-update-slice_fusion, s32[]{:T(128)S(6)} %select_n.34), kind=kLoop, calls=%fused_computation.37 | loop fusion | bytes 37748740 | tf_op jit(solution)/shard_map/jit(_roll_dynamic)/dynamic_slice | solution.py:40
  543.1 24.3 %copy.40 = bf16[384,48,512]{0,2,1:T(8,128)(2,1)} copy(bf16[384,48,512]{2,1,0:T(8,128)(2,1)} %constant_dynamic-slice_fusion) | data formatting | bytes 37748736 | tf_op jit(solution)/shard_map/jit(_roll_dynamic)/dynamic_slice | solution.py:40
  567.4 8.3 fusion.19
  575.7 1.5 fusion.21
  577.3 1.5 fusion.22
  578.8 4.7 fusion.7
  583.5 3.4 fusion.8
  587.4 2.7 copy.47
  590.2 7.0 copy.48
  597.2 106.4 %all_to_all.86 = bf16[384,48,128]{2,1,0:T(8,128)(2,1)S(1)} all-to-all(bf16[384,48,128]{2,1,0:T(8,128)(2,1)} %copy.48), channel_id=1, replica_groups=mesh['lat'=8,'chan'=4] {'lat'}, dimensions={0} | all-to-all | bytes 9437184 | tf_op jit(solution)/shard_map/all_to_all | solution.py:63
  703.6 1.4 copy.49
  704.9 10.5 %convert_bitcast_fusion = bf16[48,384,128]{1,2,0:T(8,128)(2,1)} fusion(bf16[48,384,128]{2,1,0:T(8,128)(2,1)S(1)} %bitcast.91, bf16[48,384,384]{2,1,0:T(8,128)(2,1)} %param.6), kind=kOutput, calls=%fused_computation.9 | convolution fusion | flops 1814298624 | bytes 23592960 | tf_op jit(solution)/shard_map/mlt,mlk->mtk/dot_general | solution.py:60
  715.5 7.0 copy.51
  722.5 109.3 %all_to_all.87 = bf16[48,384,128]{2,0,1:T(8,128)(2,1)} all-to-all(bf16[48,384,128]{2,0,1:T(8,128)(2,1)} %copy.51), channel_id=1, replica_groups=mesh['lat'=8,'chan'=4] {'lat'}, dimensions={1} | all-to-all | bytes 9437184 | tf_op jit(solution)/shard_map/all_to_all | solution.py:66
  831.8 12.3 %copy.67 = bf16[8,48,48,128]{1,0,3,2:T(8,128)(2,1)} copy(bf16[8,48,48,128]{3,1,2,0:T(8,128)(2,1)} %bitcast.103) | data formatting | bytes 9437184 | tf_op jit(solution)/shard_map/reshape | solution.py:67
  844.1 16.9 %reshape.100 = bf16[384,48,2,64]{0,3,2,1:T(8,128)(2,1)} reshape(bf16[8,48,48,128]{1,0,3,2:T(8,128)(2,1)} %copy.67) | data formatting | bytes 9437184 | tf_op jit(solution)/shard_map/reshape | solution.py:67
  861.1 15.5 %fusion = bf16[64,48,1024]{2,0,1:T(8,128)(2,1)S(1)} fusion(bf16[64,48,1024]{2,1,0:T(8,128)(2,1)} %param.4, bf16[384,48,2,64]{0,3,2,1:T(8,128)(2,1)} %reshape.100, bf16[1,384,1024]{2,1,0:T(8,128)(2,1)S(1)} %copy-done.6, bf16[1,384,1024]{2,1,0:T(8,128)(2,1)S(1)} %copy-done.8), kind=kOutput, calls=%fused_computation.1 | convolution fusion | flops 4844421120 | bytes 18874368 | tf_op jit(solution)/shard_map/mtrc,rmn->ctn/dot_general | solution.py:68
  876.6 6.2 copy.56
  (32 shorter events, 2.9 us)
Async XLA Ops:
  6.5 0.9 copy-start.5
  6.5 1.1 copy-start.7
  270.5 112.7 %copy-start.4 = (bf16[2,48,64,256]{3,2,1,0:T(8,128)(2,1)S(1)}, bf16[2,48,64,256]{3,2,1,0:T(8,128)(2,1)}, u32[]{:S(2)}) copy-start(bf16[2,48,64,256]{3,2,1,0:T(8,128)(2,1)} %param.7) | copy-start | bytes 9437188
  271.7 2.1 copy-start
  273.8 53.5 %collective-permute-start = (bf16[384,48,128]{2,1,0:T(8,128)(2,1)S(1)}, bf16[384,48,128]{2,1,0:T(8,128)(2,1)S(1)}, u32[]{:S(2)}, u32[]{:S(2)}) collective-permute-start(bf16[384,48,128]{2,1,0:T(8,128)(2,1)S(1)} %bitcast.86), channel_id=1, source_target_pairs={{0,1},{1,2},{2,3},{3,0},{4,5},{5,6},{6,7},{7,4},{8,9},{9,10},{10,1... | collective-permute-start | bytes 14155784 | tf_op jit(solution)/shard_map/ppermute | solution.py:39
  327.4 2.1 copy-start.2
  329.5 53.7 %collective-permute-start.1 = (bf16[384,48,128]{2,1,0:T(8,128)(2,1)S(1)}, bf16[384,48,128]{2,1,0:T(8,128)(2,1)}, u32[]{:S(2)}, u32[]{:S(2)}) collective-permute-start(bf16[384,48,128]{2,1,0:T(8,128)(2,1)S(1)} %collective-permute-done), channel_id=1, source_target_pairs={{0,1},{1,2},{2,3},{3,0},{4,5},{5,6},{6,7},{7,4},{8,9},{9,10},{10,1... | collective-permute-start | bytes 14155784 | tf_op jit(solution)/shard_map/ppermute | solution.py:39
  383.2 108.2 %collective-permute-start.2 = (bf16[384,48,128]{2,1,0:T(8,128)(2,1)}, bf16[384,48,128]{2,1,0:T(8,128)(2,1)}, u32[]{:S(2)}, u32[]{:S(2)}) collective-permute-start(bf16[384,48,128]{2,1,0:T(8,128)(2,1)} %collective-permute-done.1), channel_id=1, source_target_pairs={{0,1},{1,2},{2,3},{3,0},{4,5},{5,6},{6,7},{7,4},{8,9},{9,10},{10,1... | collective-permute-start | bytes 14155784 | tf_op jit(solution)/shard_map/ppermute | solution.py:39
  400.4 61.8 %all-to-all-start.2 = ((bf16[4,2,196608]{2,1,0:T(2,128)(2,1)}), bf16[4,2,196608]{2,1,0:T(2,128)(2,1)S(1)}, u32[]{:S(2)}, u32[]{:S(2)}) async-start(bf16[4,2,196608]{2,1,0:T(2,128)(2,1)} %reshape.101), calls=%async_computation.2 | async-start | bytes 6291456 | tf_op jit(solution)/shard_map/all_to_all | solution.py:36
  485.2 17.4 %slice-start.2 = ((s8[4718592]{0:T(1024)(128)(4,1)}), s8[524288]{0:T(1024)(128)(4,1)S(1)}, s32[]{:S(2)}) async-start(s8[4718592]{0:T(1024)(128)(4,1)} %bitcast.96), calls=%async_computation.7 | async-start | bytes 1048576
  491.4 11.2 %slice-start.3 = ((s8[4718592]{0:T(1024)(128)(4,1)}), s8[4194304]{0:T(1024)(128)(4,1)S(1)}, s32[]{:S(2)}) async-start(s8[4718592]{0:T(1024)(128)(4,1)} %bitcast.96), calls=%async_computation.8 | async-start | bytes 8388608
  497.0 8.8 slice-start
  502.6 3.2 slice-start.1
  567.4 8.3 copy-start.1
  583.5 3.4 copy-start.3
  844.1 16.9 %copy-start.6 = (bf16[1,384,1024]{2,1,0:T(8,128)(2,1)S(1)}, bf16[1,384,1024]{2,1,0:T(8,128)(2,1)}, u32[]{:S(2)}) copy-start(bf16[1,384,1024]{2,1,0:T(8,128)(2,1)} %copy-done.5) | copy-start | bytes 2359300
  844.1 16.9 %copy-start.8 = (bf16[1,384,1024]{2,1,0:T(8,128)(2,1)S(1)}, bf16[1,384,1024]{2,1,0:T(8,128)(2,1)}, u32[]{:S(2)}) copy-start(bf16[1,384,1024]{2,1,0:T(8,128)(2,1)} %copy-done.7) | copy-start | bytes 2359300
